TPU v7x, 256 devices: a whole 4x4x8 slice. The times are simulated.
256 devices in a mesh: model: 32 (over z, y), data: 8 (over x, core).
Axes of the slice: x: 4, y: 4, z: 8, core: 2. Of those that a mesh axis runs over, the one named last changes fastest.
Arguments:
- act_in: bfloat16 [65536, 1024], P('data')
- grad_out: bfloat16 [65536, 1024], P('data')
- w_up: bfloat16 [2, 1024, 4096], P(None, None, 'model')
- w_down: bfloat16 [2, 4096, 1024], P(None, 'model')
- master_up: float32 [2, 1024, 4096], P(None, 'data', 'model')
- master_down: float32 [2, 4096, 1024], P(None, ('model', 'data'))
- mom_up: float32 [2, 1024, 4096], P(None, 'data', 'model')
- mom_down: float32 [2, 4096, 1024], P(None, ('model', 'data'))
- var_up: float32 [2, 1024, 4096], P(None, 'data', 'model')
- var_down: float32 [2, 4096, 1024], P(None, ('model', 'data'))
- learn_rate: float32 [1], replicated
- clip_norm: float32 [1], replicated
Outputs:
- output 1: bfloat16 [2, 1024, 4096], P(None, None, 'model')
- output 2: bfloat16 [2, 4096, 1024], P(None, 'model')
- output 3: float32 [2, 1024, 4096], P(None, 'data', 'model')
- output 4: float32 [2, 4096, 1024], P(None, ('model', 'data'))
- output 5: float32 [2, 1024, 4096], P(None, 'data', 'model')
- output 6: float32 [2, 4096, 1024], P(None, ('model', 'data'))
- output 7: float32 [2, 1024, 4096], P(None, 'data', 'model')
- output 8: float32 [2, 4096, 1024], P(None, ('model', 'data'))
- output 9: float32 [1], replicated
All inputs are finite; a program needn't handle non-finite values.
Results may differ from a plain program's by a relative error of at most 0.00193806.
Values are sent between devices in bfloat16 or wider.
A program may use at most 768 MiB of HBM per device.

v0:
```python
import jax
import jax.numpy as jnp
from jax import lax
from jax.sharding import PartitionSpec as P

STEP = 10
BETA_ONE = 0.9
BETA_TWO = 0.95
ADAM_EPS = 1e-8
NORM_EPS = 1e-6


def gelu_fwd(z_low):
    return jax.nn.gelu(z_low.astype(jnp.float32)).astype(jnp.bfloat16)


def gelu_back(z_low, grad_low):
    _, back_fn = jax.vjp(jax.nn.gelu, z_low.astype(jnp.float32))
    return back_fn(grad_low.astype(jnp.float32))[0].astype(jnp.bfloat16)


def adam_update(master_arr, mom_arr, var_arr, grad_arr, clip_scale, lr_val):
    scaled = clip_scale * grad_arr
    new_mom = BETA_ONE * mom_arr + (1.0 - BETA_ONE) * scaled
    new_var = BETA_TWO * var_arr + (1.0 - BETA_TWO) * scaled * scaled
    mom_hat = new_mom / (1.0 - BETA_ONE ** STEP)
    var_hat = new_var / (1.0 - BETA_TWO ** STEP)
    new_master = master_arr - lr_val * mom_hat / (jnp.sqrt(var_hat) + ADAM_EPS)
    return new_master, new_mom, new_var


def local_grads(act_in, grad_out, w_up, w_down):
    z_one = jnp.dot(act_in, w_up[0], preferred_element_type=jnp.float32).astype(jnp.bfloat16)
    act_one = gelu_fwd(z_one)
    hid_part = jnp.dot(act_one, w_down[0], preferred_element_type=jnp.float32)
    hid_two = lax.psum(hid_part, "model").astype(jnp.bfloat16)
    z_two = jnp.dot(hid_two, w_up[1], preferred_element_type=jnp.float32).astype(jnp.bfloat16)
    act_two = gelu_fwd(z_two)
    grad_w4 = jnp.einsum("bf,bd->fd", act_two, grad_out, preferred_element_type=jnp.float32)
    dact_two = jnp.einsum("bd,fd->bf", grad_out, w_down[1], preferred_element_type=jnp.float32).astype(jnp.bfloat16)
    dz_two = gelu_back(z_two, dact_two)
    grad_w3 = jnp.einsum("bd,bf->df", hid_two, dz_two, preferred_element_type=jnp.float32)
    dhid_part = jnp.einsum("bf,df->bd", dz_two, w_up[1], preferred_element_type=jnp.float32)
    dhid_two = lax.psum(dhid_part, "model").astype(jnp.bfloat16)
    grad_w2 = jnp.einsum("bf,bd->fd", act_one, dhid_two, preferred_element_type=jnp.float32)
    dact_one = jnp.einsum("bd,fd->bf", dhid_two, w_down[0], preferred_element_type=jnp.float32).astype(jnp.bfloat16)
    dz_one = gelu_back(z_one, dact_one)
    grad_w1 = jnp.einsum("bd,bf->df", act_in, dz_one, preferred_element_type=jnp.float32)
    return grad_w1, grad_w3, grad_w2, grad_w4


def solution(mesh):
    data_size = mesh.shape["data"]
    spec_rows = P("data", None)
    spec_wup = P(None, None, "model")
    spec_wdown = P(None, "model", None)
    spec_sup = P(None, "data", "model")
    spec_sdown = P(None, ("model", "data"), None)
    spec_scalar = P(None)

    def local_step(act_in, grad_out, w_up, w_down, master_up, master_down, mom_up, mom_down, var_up, var_down, learn_rate, clip_norm):
        grad_w1, grad_w3, grad_w2, grad_w4 = local_grads(act_in, grad_out, w_up, w_down)
        shard_w4 = lax.psum_scatter(grad_w4, "data", scatter_dimension=0, tiled=True)
        shard_w3 = lax.psum_scatter(grad_w3, "data", scatter_dimension=0, tiled=True)
        shard_w2 = lax.psum_scatter(grad_w2, "data", scatter_dimension=0, tiled=True)
        shard_w1 = lax.psum_scatter(grad_w1, "data", scatter_dimension=0, tiled=True)
        grad_up = jnp.stack([shard_w1, shard_w3]) / data_size
        grad_down = jnp.stack([shard_w2, shard_w4]) / data_size
        sq_local = jnp.sum(grad_up * grad_up) + jnp.sum(grad_down * grad_down)
        norm_val = jnp.sqrt(lax.psum(sq_local, ("model", "data")))
        clip_scale = jnp.minimum(1.0, clip_norm[0] / (norm_val + NORM_EPS))
        lr_val = learn_rate[0]
        new_master_up, new_mom_up, new_var_up = adam_update(master_up, mom_up, var_up, grad_up, clip_scale, lr_val)
        new_master_down, new_mom_down, new_var_down = adam_update(master_down, mom_down, var_down, grad_down, clip_scale, lr_val)
        new_w_up = lax.all_gather(new_master_up.astype(jnp.bfloat16), "data", axis=1, tiled=True)
        new_w_down = lax.all_gather(new_master_down.astype(jnp.bfloat16), "data", axis=1, tiled=True)
        return (new_w_up, new_w_down, new_master_up, new_master_down, new_mom_up, new_mom_down, new_var_up, new_var_down, norm_val.reshape(1))

    return jax.shard_map(local_step, mesh=mesh, in_specs=(spec_rows, spec_rows, spec_wup, spec_wdown, spec_sup, spec_sdown, spec_sup, spec_sdown, spec_sup, spec_sdown, spec_scalar, spec_scalar), out_specs=(spec_wup, spec_wdown, spec_sup, spec_sdown, spec_sup, spec_sdown, spec_sup, spec_sdown, spec_scalar), check_vma=False)
```

profile of v0, /device:TPU:1, one launch (start us, length us, event | category | flops | bytes accessed | tf_op | source)
XLA Modules:
  0.0 1764.9 jit_solution(2158154898176052643)
XLA Ops:
  7.2 8.3 fusion.1
  15.6 2.0 copy-done
  17.6 13.1 fusion.51
  30.7 729.8 %all-reduce.2 = bf16[8192,1024]{1,0:T(8,128)(2,1)} all-reduce(f32[8192,1024]{1,0:T(8,128)} %fusion.51), channel_id=1, replica_groups=mesh['model'=32,'data'=8] {'model'}, use_global_device_ids=true, to_apply=%region_0.0 | all-reduce | flops 8388608 | bytes 50331648 | tf_op jit(solution)/shard_map/psum | solution.py:36
  760.6 10.0 fusion.2
  770.6 11.1 fusion.23
  781.7 3.4 fusion.78
  785.2 13.2 fusion.46
  798.3 722.1 %all-reduce.3 = bf16[8192,1024]{1,0:T(8,128)(2,1)} all-reduce(f32[8192,1024]{1,0:T(8,128)} %fusion.46), channel_id=1, replica_groups=mesh['model'=32,'data'=8] {'model'}, use_global_device_ids=true, to_apply=%region_1.0 | all-reduce | flops 8388608 | bytes 50331648 | tf_op jit(solution)/shard_map/psum | solution.py:44
  1520.5 17.9 %fusion.43 = f32[1024,128]{0,1:T(8,128)} fusion(bf16[8192,1024]{1,0:T(8,128)(2,1)} %param.12, f32[8192,128]{1,0:T(8,128)} %copy-done, bf16[8192,1024]{1,0:T(8,128)(2,1)} %all-reduce.3, bf16[2,128,1024]{2,1,0:T(8,128)(2,1)S(1)} %copy-done.3), kind=kOutput, calls=%fused_computation.48 | convolution fusion | flops 4318035968 | bytes 38535168 | tf_op jit(solution)/shard_map/bd,bf->df/dot_general | solution.py:48
  1538.5 11.3 fusion.32
  1550.2 11.3 fusion.4
  1563.1 7.6 reduce-scatter.5.cloned.1.call-done
  1570.7 1.5 multiply_reduce_fusion.1
  1572.2 33.8 %reduce-scatter.11.cloned.1.call-done = f32[16,1024]{1,0:T(8,128)} async-done(((f32[128,1024]{1,0:T(8,128)}), f32[16,1024]{1,0:T(8,128)}) %reduce-scatter.11.cloned.1.call-update) | async-done | bytes 65552 | tf_op jit(solution)/shard_map/reduce_scatter | solution.py:63
  1606.1 35.1 %reduce-scatter.9.cloned.1.call-done = f32[16,1024]{1,0:T(8,128)} async-done(((f32[128,1024]{1,0:T(8,128)}), f32[16,1024]{1,0:T(8,128)}) %reduce-scatter.9.cloned.1.call-update) | async-done | bytes 65552 | tf_op jit(solution)/shard_map/reduce_scatter | solution.py:65
  1641.2 1.5 multiply_reduce_fusion
  1644.0 78.2 %psum.23 = f32[]{:T(128)} all-reduce(f32[]{:T(128)S(6)} %add.66), channel_id=1, replica_groups=mesh['model'=32,'data'=8] {'model','data'}, use_global_device_ids=true, to_apply=%region_8.0 | all-reduce | flops 1 | bytes 8 | tf_op jit(solution)/shard_map/psum | solution.py:70
  1723.0 1.0 fusion.76
  1726.2 1.7 fusion.74
  1727.9 13.8 all_gather.7
  1741.7 13.7 all_gather.6
  1755.5 1.0 copy.25
  1756.5 0.8 copy.37
  (43 shorter events, 3.1 us)
Async XLA Ops:
  7.2 10.4 copy-start.3
  7.2 1555.9 %reduce-scatter.7.cloned.1.call-start = ((), (), s32[]{:S(2)}) async-start(), calls=%async_computation.5 | async-start | bytes 589824 | tf_op jit(solution)/shard_map/reduce_scatter | solution.py:64
  15.6 2.0 copy-start
  30.7 729.8 %copy-start.2 = (bf16[2,1024,128]{2,1,0:T(8,128)(2,1)S(1)}, bf16[2,1024,128]{2,1,0:T(8,128)(2,1)}, u32[]{:S(2)}) copy-start(bf16[2,1024,128]{2,1,0:T(8,128)(2,1)} %param.14) | copy-start | bytes 1572868
  760.5 21.1 %slice-start = ((s8[16777216]{0:T(1024)(128)(4,1)}), s8[4194304]{0:T(1024)(128)(4,1)S(1)}, s32[]{:S(2)}) async-start(s8[16777216]{0:T(1024)(128)(4,1)} %bitcast.37), calls=%async_computation.8 | async-start | bytes 8388608
  760.5 21.1 %slice-start.1 = ((s8[16777216]{0:T(1024)(128)(4,1)}), s8[4194304]{0:T(1024)(128)(4,1)S(1)}, s32[]{:S(2)}) async-start(s8[16777216]{0:T(1024)(128)(4,1)} %bitcast.37), calls=%async_computation.9 | async-start | bytes 8388608
  770.6 11.1 copy-start.1
  770.6 11.1 slice-start.2
  770.6 11.1 slice-start.3
  785.1 785.6 %reduce-scatter.5.cloned.1.call-start = ((), (), s32[]{:S(2)}) async-start(), calls=%async_computation.4 | async-start | bytes 589824 | tf_op jit(solution)/shard_map/reduce_scatter | solution.py:66
  1538.4 67.6 %reduce-scatter.11.cloned.1.call-start = ((), (), s32[]{:S(2)}) async-start(), calls=%async_computation.7 | async-start | bytes 589824 | tf_op jit(solution)/shard_map/reduce_scatter | solution.py:63
  1549.8 13.0 copy-start.7
  1549.8 13.1 copy-start.8
  1549.8 13.2 copy-start.9
  1549.8 176.4 %copy-start.4 = (f32[2,16,1024]{2,1,0:T(8,128)S(1)}, f32[2,16,1024]{2,1,0:T(8,128)}, u32[]{:S(2)}) copy-start(f32[2,16,1024]{2,1,0:T(8,128)} %param.17) | copy-start | bytes 393220
  1549.8 176.4 %copy-start.5 = (f32[2,16,1024]{2,1,0:T(8,128)S(1)}, f32[2,16,1024]{2,1,0:T(8,128)}, u32[]{:S(2)}) copy-start(f32[2,16,1024]{2,1,0:T(8,128)} %param.19) | copy-start | bytes 393220
  1549.8 176.4 %copy-start.6 = (f32[2,16,1024]{2,1,0:T(8,128)S(1)}, f32[2,16,1024]{2,1,0:T(8,128)}, u32[]{:S(2)}) copy-start(f32[2,16,1024]{2,1,0:T(8,128)} %param.21) | copy-start | bytes 393220
  1549.9 91.4 %reduce-scatter.9.cloned.1.call-start = ((), (), s32[]{:S(2)}) async-start(), calls=%async_computation.6 | async-start | bytes 589824 | tf_op jit(solution)/shard_map/reduce_scatter | solution.py:65
Sparse Core Ops, SparseCore 0:
  785.3 31.3 reduce-scatter.6
  1538.5 32.1 reduce-scatter.4
  1573.3 32.7 reduce-scatter.10
  1608.4 32.7 reduce-scatter.8
where the time goes:
time: 1770 us; the launch traced here: 1760 us
  blocking collectives  1560 us (88%)
  matrix products  99.5 us (6%)
  waiting for transfers between devices  76.6 us (4%)
  between operations  18.5 us (1%)
    psum x1, blocking collectives, local_grads(): hid_two = lax.psum(hid_part, 'model').astype(jnp.bfloat16)  730 us
    psum x1, blocking collectives, local_grads(): dhid_two = lax.psum(dhid_part, 'model').astype(jnp.bfloat16)  722 us
    psum x1, blocking collectives, local_step(): norm_val = jnp.sqrt(lax.psum(sq_local, ('model', 'data')))  78.2 us
  transfers between devices with their start and end apart: 4, of which 3 were waited for; matrix products, arithmetic and copies ran while one was open for 3% of the time, Pallas kernels for 0%

commit v1 on v0

v1 whole, which is shorter than its diff:
```python
import jax
import jax.numpy as jnp
from jax import lax
from jax.sharding import Mesh, PartitionSpec as P

STEP = 10
BETA_ONE = 0.9
BETA_TWO = 0.95
ADAM_EPS = 1e-8
NORM_EPS = 1e-6
F32 = jnp.float32
BF16 = jnp.bfloat16


def gelu_fwd(z_low):
    return jax.nn.gelu(z_low.astype(F32)).astype(BF16)


def gelu_back(z_low, grad_low):
    _, back_fn = jax.vjp(jax.nn.gelu, z_low.astype(F32))
    return back_fn(grad_low.astype(F32))[0].astype(BF16)


def adam_update(master_arr, mom_arr, var_arr, grad_arr, clip_scale, lr_val):
    scaled = clip_scale * grad_arr
    new_mom = BETA_ONE * mom_arr + (1.0 - BETA_ONE) * scaled
    new_var = BETA_TWO * var_arr + (1.0 - BETA_TWO) * scaled * scaled
    mom_hat = new_mom / (1.0 - BETA_ONE ** STEP)
    var_hat = new_var / (1.0 - BETA_TWO ** STEP)
    new_master = master_arr - lr_val * mom_hat / (jnp.sqrt(var_hat) + ADAM_EPS)
    return new_master, new_mom, new_var


def dot_nt(left, right):
    return lax.dot_general(left, right, (((1,), (1,)), ((), ())), preferred_element_type=F32)


def dot_nn(left, right):
    return lax.dot_general(left, right, (((1,), (0,)), ((), ())), preferred_element_type=F32)


def dot_tn(left, right):
    return lax.dot_general(left, right, (((0,), (0,)), ((), ())), preferred_element_type=F32)


def sum_rows(part):
    mine = lax.psum_scatter(part, "y", scatter_dimension=0, tiled=True).astype(BF16)
    return lax.all_gather(mine, "y", axis=0, tiled=True)


def solution(mesh):
    big = Mesh(mesh.devices.reshape(8, 4, 4, 2), ("z", "y", "x", "c"))
    model = ("z", "y")
    data = ("x", "c")
    spec_rows = P(data, None)
    spec_wup = P(None, None, model)
    spec_wdown = P(None, model, None)
    spec_sup = P(None, data, model)
    spec_sdown = P(None, model + data, None)
    spec_scalar = P(None)

    def local_step(act_in, grad_out, w_up, w_down, master_up, master_down, mom_up, mom_down, var_up, var_down, learn_rate, clip_norm):
        rows = act_in.shape[0] // 8
        start = lax.axis_index("z") * rows
        x_loc = lax.dynamic_slice_in_dim(act_in, start, rows, 0)
        dy_loc = lax.dynamic_slice_in_dim(grad_out, start, rows, 0)
        up_t = jnp.swapaxes(w_up, 1, 2)
        w1t = lax.all_gather(up_t[0], "z", axis=0, tiled=True)
        w2 = lax.all_gather(w_down[0], "z", axis=0, tiled=True)
        w3t = lax.all_gather(up_t[1], "z", axis=0, tiled=True)
        w4 = lax.all_gather(w_down[1], "z", axis=0, tiled=True)
        z_one = dot_nt(x_loc, w1t).astype(BF16)
        act_one = gelu_fwd(z_one)
        hid = sum_rows(dot_nn(act_one, w2))
        z_two = dot_nt(hid, w3t).astype(BF16)
        act_two = gelu_fwd(z_two)
        g4 = dot_tn(act_two, dy_loc)
        dz_two = gelu_back(z_two, dot_nt(dy_loc, w4).astype(BF16))
        g3 = dot_tn(dz_two, hid)
        err = sum_rows(dot_nn(dz_two, w3t))
        g2 = dot_tn(act_one, err)
        dz_one = gelu_back(z_one, dot_nt(err, w2).astype(BF16))
        g1 = dot_tn(dz_one, x_loc)
        every = ("z", "x", "c")

        def red_down(grad):
            return lax.psum_scatter(grad, every, scatter_dimension=0, tiled=True)

        def red_up(grad):
            blocks = grad.reshape(8, 128, 8, 128).transpose(0, 2, 1, 3).reshape(64 * 128, 128)
            return lax.psum_scatter(blocks, every, scatter_dimension=0, tiled=True).T

        grad_down = jnp.stack([red_down(g2), red_down(g4)]) / 8
        grad_up = jnp.stack([red_up(g1), red_up(g3)]) / 8
        sq_local = jnp.sum(grad_up * grad_up) + jnp.sum(grad_down * grad_down)
        norm_val = jnp.sqrt(lax.psum(sq_local, ("z", "y", "x", "c")))
        clip_scale = jnp.minimum(1.0, clip_norm[0] / (norm_val + NORM_EPS))
        lr_val = learn_rate[0]
        new_master_up, new_mom_up, new_var_up = adam_update(master_up, mom_up, var_up, grad_up, clip_scale, lr_val)
        new_master_down, new_mom_down, new_var_down = adam_update(master_down, mom_down, var_down, grad_down, clip_scale, lr_val)
        new_w_up = lax.all_gather(new_master_up.astype(BF16), data, axis=1, tiled=True)
        new_w_down = lax.all_gather(new_master_down.astype(BF16), data, axis=1, tiled=True)
        return (new_w_up, new_w_down, new_master_up, new_master_down, new_mom_up, new_mom_down, new_var_up, new_var_down, norm_val.reshape(1))

    return jax.shard_map(local_step, mesh=big, in_specs=(spec_rows, spec_rows, spec_wup, spec_wdown, spec_sup, spec_sdown, spec_sup, spec_sdown, spec_sup, spec_sdown, spec_scalar, spec_scalar), out_specs=(spec_wup, spec_wdown, spec_sup, spec_sdown, spec_sup, spec_sdown, spec_sup, spec_sdown, spec_scalar), check_vma=False)
```

time: 1770 us -> 1090 us (0.62)
  blocking collectives: 1560 us -> 106 us
  waiting for transfers between devices: 76.6 us -> 846 us
  matrix products: 99.5 us -> 56.7 us
  local copies, waits for them, and re-layouts: 6.44 us -> 44 us
    psum x3 -> x1, blocking collectives: 1530 us -> 79.6 us  [local_step(): norm_val = jnp.sqrt(lax.psum(sq_local, ('z', 'y', 'x', 'c')))]
    reduce_scatter x4 -> x6, waiting for transfers between devices: 76.6 us -> 638 us  [the longest x2 292 us: red_down(): return lax.psum_scatter(grad, every, scatter_dimension=0, tiled=True)]
    all_gather x0 -> x6, waiting for transfers between devices: none -> 207 us  [the longest x2 51.1 us: sum_rows(): return lax.all_gather(mine, 'y', axis=0, tiled=True)]
    dot_general x9, matrix products: 99.5 us -> 56.7 us  [the longest x4 28.3 us: dot_tn(): lax.dot_general(left, right, (((0,), (0,)), ((), ())), preferred_element_...]
    unnamed x36 -> x32, local copies, waits for them, and re-layouts: 6.44 us -> 24.9 us
  transfers between devices with their start and end apart: 4 -> 12, of which waited for: 3 -> 12; matrix products, arithmetic and copies ran while one was open for 3% -> 7% of each run, Pallas kernels for 0% -> 0%
where the time goes in v1:
time: 1090 us; the launch traced here: 1080 us
  waiting for transfers between devices  846 us (78%)
  blocking collectives  106 us (10%)
  matrix products  56.7 us (5%)
  local copies, waits for them, and re-layouts  44 us (4%)
  between operations  19.1 us (2%)
    reduce_scatter x2, waiting for transfers between devices, red_down(): return lax.psum_scatter(grad, every, scatter_dimension=0, tiled=True)  292 us
    reduce_scatter x2, waiting for transfers between devices, red_up(): return lax.psum_scatter(blocks, every, scatter_dimension=0, tiled=True).T  243 us
    reduce_scatter x2, waiting for transfers between devices, sum_rows(): lax.psum_scatter(part, 'y', scatter_dimension=0, tiled=True).astype(BF16)  103 us
    psum x1, blocking collectives, local_step(): norm_val = jnp.sqrt(lax.psum(sq_local, ('z', 'y', 'x', 'c')))  79.6 us
    all_gather x2, waiting for transfers between devices, sum_rows(): return lax.all_gather(mine, 'y', axis=0, tiled=True)  51.1 us
    all_gather x1, waiting for transfers between devices, local_step(): w1t = lax.all_gather(up_t[0], 'z', axis=0, tiled=True)  44.8 us
    all_gather x1, waiting for transfers between devices, local_step(): w3t = lax.all_gather(up_t[1], 'z', axis=0, tiled=True)  40.7 us
    all_gather x1, waiting for transfers between devices, local_step(): w2 = lax.all_gather(w_down[0], 'z', axis=0, tiled=True)  37.7 us
  transfers between devices with their start and end apart: 12, of which 12 were waited for; matrix products, arithmetic and copies ran while one was open for 7% of the time, Pallas kernels for 0%

profile of v1, /device:TPU:1, one launch (start us, length us, event | category | flops | bytes accessed | tf_op | source)
XLA Modules:
  0.0 1084.7 jit_solution(6818606660254951167)
XLA Ops:
  11.1 44.8 %all-gather.17.cloned.1.call-done = bf16[1,1024,1024]{1,2,0:T(8,128)(2,1)} async-done(((bf16[1,128,1024]{1,2,0:T(8,128)(2,1)}), bf16[1,1024,1024]{1,2,0:T(8,128)(2,1)}) %all-gather.17.cloned.1.call-update) | async-done | bytes 2097168 | tf_op jit(solution)/shard_map/all_gather | solution.py:68
  60.5 37.7 %all-gather.19.cloned.1.call-done = bf16[1,1024,1024]{2,1,0:T(8,128)(2,1)} async-done(((bf16[1,128,1024]{2,1,0:T(8,128)(2,1)}), bf16[1,1024,1024]{2,1,0:T(8,128)(2,1)}) %all-gather.19.cloned.1.call-update) | async-done | bytes 2097168 | tf_op jit(solution)/shard_map/all_gather | solution.py:69
  98.2 6.3 fusion.30
  105.1 51.4 %reduce-scatter.7.cloned.1.call-done = f32[256,1024]{1,0:T(8,128)} async-done(((f32[1024,1024]{1,0:T(8,128)}), f32[256,1024]{1,0:T(8,128)}) %reduce-scatter.7.cloned.1.call-update) | async-done | bytes 1048592 | tf_op jit(solution)/shard_map/reduce_scatter | solution.py:47
  159.8 40.7 %all-gather.21.cloned.1.call-done = bf16[1,1024,1024]{1,2,0:T(8,128)(2,1)} async-done(((bf16[1,128,1024]{1,2,0:T(8,128)(2,1)}), bf16[1,1024,1024]{1,2,0:T(8,128)(2,1)}) %all-gather.21.cloned.1.call-update) | async-done | bytes 2097168 | tf_op jit(solution)/shard_map/all_gather | solution.py:70
  200.5 38.6 %all-gather.11.cloned.1.call-done = bf16[1024,1024]{1,0:T(8,128)(2,1)} async-done(((bf16[256,1024]{1,0:T(8,128)(2,1)}), bf16[1024,1024]{1,0:T(8,128)(2,1)}) %all-gather.11.cloned.1.call-update) | async-done | bytes 2097168 | tf_op jit(solution)/shard_map/all_gather | solution.py:48
  239.0 5.9 fusion.52
  244.9 33.1 %all-gather.15.cloned.1.call-done = bf16[1,1024,1024]{2,1,0:T(8,128)(2,1)} async-done(((bf16[1,128,1024]{2,1,0:T(8,128)(2,1)}), bf16[1,1024,1024]{2,1,0:T(8,128)(2,1)}) %all-gather.15.cloned.1.call-update) | async-done | bytes 2097168 | tf_op jit(solution)/shard_map/all_gather | solution.py:71
  278.0 7.5 fusion.4
  291.2 52.0 %reduce-scatter.9.cloned.1.call-done = f32[256,1024]{1,0:T(8,128)} async-done(((f32[1024,1024]{1,0:T(8,128)}), f32[256,1024]{1,0:T(8,128)}) %reduce-scatter.9.cloned.1.call-update) | async-done | bytes 1048592 | tf_op jit(solution)/shard_map/reduce_scatter | solution.py:47
  352.7 5.4 copy.22
  358.2 7.4 copy.29
  365.8 12.6 %all-gather.13.cloned.1.call-done = bf16[1024,1024]{1,0:T(8,128)(2,1)} async-done(((bf16[256,1024]{1,0:T(8,128)(2,1)}), bf16[1024,1024]{1,0:T(8,128)(2,1)}) %all-gather.13.cloned.1.call-update) | async-done | bytes 2097168 | tf_op jit(solution)/shard_map/all_gather | solution.py:48
  378.4 11.3 %convolution_bitcast_fusion.1 = f32[128,8,8,128]{3,1,2,0:T(8,128)} fusion(bf16[1024,1024]{1,0:T(8,128)(2,1)} %copy-done.12, bf16[8192,1024]{1,0:T(8,128)(2,1)} %param.12, s32[]{:T(128)S(6)} %select_n.4, bf16[1024,1024]{1,0:T(8,128)(2,1)} %all-gather.13.cloned.1.call-done, bf16[1,1024,1024]{2,1,0:T(8,128)(2,1)S(1)} %copy-done.6), kind=kOutput, calls=%fused_computation.39 | convolution fusion | flops 4319084544 | bytes 12582916 | tf_op jit(solution)/shard_map/dot_general | solution.py:43
  400.7 7.5 copy.30
  409.7 6.5 fusion.22
  417.8 6.5 fusion.79
  425.8 96.0 %reduce-scatter.13.cloned.1.call-done = f32[128,128]{0,1:T(8,128)} async-done(((f32[8192,128]{0,1:T(8,128)}), f32[128,128]{0,1:T(8,128)}) %reduce-scatter.13.cloned.1.call-update) | async-done | bytes 65552 | tf_op jit(solution)/shard_map/reduce_scatter | solution.py:91
  521.8 146.5 %reduce-scatter.11.cloned.1.call-done = f32[128,128]{0,1:T(8,128)} async-done(((f32[8192,128]{0,1:T(8,128)}), f32[128,128]{0,1:T(8,128)}) %reduce-scatter.11.cloned.1.call-update) | async-done | bytes 65552 | tf_op jit(solution)/shard_map/reduce_scatter | solution.py:91
  669.9 145.2 %reduce-scatter.17.cloned.1.call-done = f32[16,1024]{1,0:T(8,128)} async-done(((f32[1024,1024]{1,0:T(8,128)}), f32[16,1024]{1,0:T(8,128)}) %reduce-scatter.17.cloned.1.call-update) | async-done | bytes 65552 | tf_op jit(solution)/shard_map/reduce_scatter | solution.py:87
  815.1 146.6 %reduce-scatter.15.cloned.1.call-done = f32[16,1024]{1,0:T(8,128)} async-done(((f32[1024,1024]{1,0:T(8,128)}), f32[16,1024]{1,0:T(8,128)}) %reduce-scatter.15.cloned.1.call-update) | async-done | bytes 65552 | tf_op jit(solution)/shard_map/reduce_scatter | solution.py:87
  964.5 79.6 %psum.7 = f32[]{:T(128)} all-reduce(f32[]{:T(128)S(6)} %add.71), channel_id=1, replica_groups=mesh['z'=8,'y'=4,'x'=4,'c'=2] {'z','y','x','c'}, use_global_device_ids=true, to_apply=%region_8.0 | all-reduce | flops 1 | bytes 8 | tf_op jit(solution)/shard_map/psum | solution.py:96
  1046.6 13.6 %all_gather.30 = bf16[2,1024,128]{2,1,0:T(8,128)(2,1)S(1)} all-gather(bf16[2,128,128]{2,1,0:T(8,128)(2,1)S(1)} %get-tuple-element.13), channel_id=1, replica_groups=mesh['z'=8,'y'=4,'x'=4,'c'=2] {'x','c'}, dimensions={1}, use_global_device_ids=true | all-gather | bytes 589824 | tf_op jit(solution)/shard_map/all_gather | solution.py:101
  1061.8 13.1 %all_gather.31 = bf16[2,128,1024]{2,1,0:T(8,128)(2,1)S(1)} all-gather(bf16[2,16,1024]{2,1,0:T(8,128)(2,1)S(1)} %get-tuple-element.9), channel_id=1, replica_groups=mesh['z'=8,'y'=4,'x'=4,'c'=2] {'x','c'}, dimensions={1}, use_global_device_ids=true | all-gather | bytes 589824 | tf_op jit(solution)/shard_map/all_gather | solution.py:102
  (68 shorter events, 49.9 us)
Async XLA Ops:
  7.2 48.8 %all-gather.17.cloned.1.call-start = ((), (), s32[]{:S(2)}) async-start(), calls=%async_computation.15 | async-start | bytes 2359296 | tf_op jit(solution)/shard_map/all_gather | solution.py:68
  9.1 89.0 %all-gather.19.cloned.1.call-start = ((), (), s32[]{:S(2)}) async-start(), calls=%async_computation.16 | async-start | bytes 2359296 | tf_op jit(solution)/shard_map/all_gather | solution.py:69
  11.0 145.4 %reduce-scatter.7.cloned.1.call-start = ((), (), s32[]{:S(2)}) async-start(), calls=%async_computation.6 | async-start | bytes 5242880 | tf_op jit(solution)/shard_map/reduce_scatter | solution.py:47
  60.5 44.0 %copy-start.12 = (bf16[1024,1024]{1,0:T(8,128)(2,1)}, bf16[1024,1024]{1,0:T(8,128)(2,1)S(1)}, u32[]{:S(2)}) copy-start(bf16[1024,1024]{1,0:T(8,128)(2,1)S(1)} %fusion.49) | copy-start | bytes 6291460
  104.5 96.0 %all-gather.21.cloned.1.call-start = ((), (), s32[]{:S(2)}) async-start(), calls=%async_computation.17 | async-start | bytes 2359296 | tf_op jit(solution)/shard_map/all_gather | solution.py:70
  105.0 134.0 %all-gather.11.cloned.1.call-start = ((), (), s32[]{:S(2)}) async-start(), calls=%async_computation.7 | async-start | bytes 2621440 | tf_op jit(solution)/shard_map/all_gather | solution.py:48
  158.6 119.4 %all-gather.15.cloned.1.call-start = ((), (), s32[]{:S(2)}) async-start(), calls=%async_computation.14 | async-start | bytes 2359296 | tf_op jit(solution)/shard_map/all_gather | solution.py:71
  159.2 184.0 %reduce-scatter.9.cloned.1.call-start = ((), (), s32[]{:S(2)}) async-start(), calls=%async_computation.8 | async-start | bytes 5242880 | tf_op jit(solution)/shard_map/reduce_scatter | solution.py:47
  244.9 41.9 %copy-start.9 = (bf16[1,1024,1024]{1,2,0:T(8,128)(2,1)S(1)}, bf16[1,1024,1024]{1,2,0:T(8,128)(2,1)}, u32[]{:S(2)}) copy-start(bf16[1,1024,1024]{1,2,0:T(8,128)(2,1)} %all-gather.21.cloned.1.call-done) | copy-start | bytes 6291460
  291.1 54.4 %copy-start.8 = (bf16[1024,1024]{1,0:T(8,128)(2,1)S(1)}, bf16[1024,1024]{1,0:T(8,128)(2,1)}, u32[]{:S(2)}) copy-start(bf16[1024,1024]{1,0:T(8,128)(2,1)} %all-gather.11.cloned.1.call-done) | copy-start | bytes 6291460
  291.1 87.3 %all-gather.13.cloned.1.call-start = ((), (), s32[]{:S(2)}) async-start(), calls=%async_computation.9 | async-start | bytes 2621440 | tf_op jit(solution)/shard_map/all_gather | solution.py:48
  345.3 176.5 %reduce-scatter.13.cloned.1.call-start = ((), (), s32[]{:S(2)}) async-start(), calls=%async_computation.11 | async-start | bytes 4259840 | tf_op jit(solution)/shard_map/reduce_scatter | solution.py:91
  365.6 12.9 %copy-start.6 = (bf16[1,1024,1024]{2,1,0:T(8,128)(2,1)S(1)}, bf16[1,1024,1024]{2,1,0:T(8,128)(2,1)}, u32[]{:S(2)}) copy-start(bf16[1,1024,1024]{2,1,0:T(8,128)(2,1)} %all-gather.19.cloned.1.call-done) | copy-start | bytes 6291460
  365.6 302.8 %reduce-scatter.11.cloned.1.call-start = ((), (), s32[]{:S(2)}) async-start(), calls=%async_computation.10 | async-start | bytes 4259840 | tf_op jit(solution)/shard_map/reduce_scatter | solution.py:91
  408.1 1.6 copy-start.11
  408.2 406.9 %reduce-scatter.17.cloned.1.call-start = ((), (), s32[]{:S(2)}) async-start(), calls=%async_computation.13 | async-start | bytes 4259840 | tf_op jit(solution)/shard_map/reduce_scatter | solution.py:87
  416.3 1.6 copy-start.7
  416.3 545.5 %reduce-scatter.15.cloned.1.call-start = ((), (), s32[]{:S(2)}) async-start(), calls=%async_computation.12 | async-start | bytes 4259840 | tf_op jit(solution)/shard_map/reduce_scatter | solution.py:87
  424.3 620.5 %copy-start = (f32[2,128,128]{2,1,0:T(8,128)S(1)}, f32[2,128,128]{2,1,0:T(8,128)}, u32[]{:S(2)}) copy-start(f32[2,128,128]{2,1,0:T(8,128)} %param.16) | copy-start | bytes 393220
  424.3 620.5 %copy-start.1 = (f32[2,128,128]{2,1,0:T(8,128)S(1)}, f32[2,128,128]{2,1,0:T(8,128)}, u32[]{:S(2)}) copy-start(f32[2,128,128]{2,1,0:T(8,128)} %param.18) | copy-start | bytes 393220
  424.3 620.5 %copy-start.2 = (f32[2,128,128]{2,1,0:T(8,128)S(1)}, f32[2,128,128]{2,1,0:T(8,128)}, u32[]{:S(2)}) copy-start(f32[2,128,128]{2,1,0:T(8,128)} %param.20) | copy-start | bytes 393220
  424.4 635.8 %copy-start.3 = (f32[2,16,1024]{2,1,0:T(8,128)S(1)}, f32[2,16,1024]{2,1,0:T(8,128)}, u32[]{:S(2)}) copy-start(f32[2,16,1024]{2,1,0:T(8,128)} %param.17) | copy-start | bytes 393220
  424.4 635.8 %copy-start.4 = (f32[2,16,1024]{2,1,0:T(8,128)S(1)}, f32[2,16,1024]{2,1,0:T(8,128)}, u32[]{:S(2)}) copy-start(f32[2,16,1024]{2,1,0:T(8,128)} %param.19) | copy-start | bytes 393220
  424.4 635.8 %copy-start.5 = (f32[2,16,1024]{2,1,0:T(8,128)S(1)}, f32[2,16,1024]{2,1,0:T(8,128)}, u32[]{:S(2)}) copy-start(f32[2,16,1024]{2,1,0:T(8,128)} %param.21) | copy-start | bytes 393220
  (1 other events, 1.4 us)
Sparse Core Ops, SparseCore 0:
  9.7 46.1 all-gather.16
  58.3 39.8 all-gather.18
  104.6 51.8 reduce-scatter.6
  158.1 42.3 all-gather.20
  202.7 36.2 all-gather.10
  241.3 36.6 all-gather.14
  291.2 51.8 reduce-scatter.8
  345.5 32.8 all-gather.12
  382.6 139.2 reduce-scatter.12
  525.8 142.5 reduce-scatter.10
  672.5 142.5 reduce-scatter.16
  819.1 142.6 reduce-scatter.14

commit v2 on v1

v2 whole, which is shorter than its diff:
```python
import jax
import jax.numpy as jnp
from jax import lax
from jax.experimental import pallas as pl
from jax.experimental.pallas import tpu as pltpu
from jax.sharding import Mesh, PartitionSpec as P

STEP = 10
BETA_ONE = 0.9
BETA_TWO = 0.95
ADAM_EPS = 1e-8
NORM_EPS = 1e-6
F32 = jnp.float32
BF16 = jnp.bfloat16
MESH = pl.DeviceIdType.MESH
ROOT = 0.7978845608028654
CUBE = 0.044715
VMEM_LIMIT = 67043328
WIDE = 1024
LANE = 128
SPAN = 512
TILE = 256
HALF = 64
SUB = 16
EIGHT = 8
FOUR = 4
PAIR = 2
TRIO = 3
SEVEN = 7
HALFROW = 32
SIX = 6


def nn(left, right):
    return lax.dot_general(left, right, (((1,), (0,)), ((), ())), preferred_element_type=F32)


def nt(left, right):
    return lax.dot_general(left, right, (((1,), (1,)), ((), ())), preferred_element_type=F32)


def tn(left, right):
    return lax.dot_general(left, right, (((0,), (0,)), ((), ())), preferred_element_type=F32)


def gelu_val(z):
    t = jnp.tanh(ROOT * (z + CUBE * (z * z * z)))
    return z * (0.5 * (1.0 + t))


def gelu_both(z):
    sq = z * z
    t = jnp.tanh(ROOT * (z + CUBE * (sq * z)))
    half = 0.5 * (1.0 + t)
    slope = half + z * (0.5 * (1.0 - t * t)) * (ROOT * (1.0 + (3.0 * CUBE) * sq))
    return z * half, slope


def adam_update(master_arr, mom_arr, var_arr, grad_arr, clip_scale, lr_val):
    scaled = clip_scale * grad_arr
    new_mom = BETA_ONE * mom_arr + (1.0 - BETA_ONE) * scaled
    new_var = BETA_TWO * var_arr + (1.0 - BETA_TWO) * scaled * scaled
    mom_hat = new_mom / (1.0 - BETA_ONE ** STEP)
    var_hat = new_var / (1.0 - BETA_TWO ** STEP)
    new_master = master_arr - lr_val * mom_hat / (jnp.sqrt(var_hat) + ADAM_EPS)
    return new_master, new_mom, new_var


def kernel(
    act_ref, dy_ref, wup_ref, wdn_ref, up_ref_a, up_ref_b, up_ref_c, down_ref_a, down_ref_b, down_ref_c, lr_ref, clip_ref,
    grad_out_ref, norm_out_ref, weight_out_ref,
    X, DY, W, Z1, A1, Z3, A3, H, E2, Q3, PART, Y1, Y2, G, DD, X1, X2, ZS, ZR, NW, NSRC, NRCV, NRCW, SUP, SDN, GOUT, NOUT,
    local_sem, send_sem, recv_sem, credit,
):
    z = lax.axis_index("z")
    y = lax.axis_index("y")
    x = lax.axis_index("x")
    c = lax.axis_index("c")
    other = 1 - c
    used = {"send": 0, "recv": 0}

    def recv_id():
        used["recv"] += 1
        return used["recv"] - 1

    def send(src, dst, rid, where):
        sid = used["send"]
        used["send"] += 1
        copy = pltpu.make_async_remote_copy(src_ref=src, dst_ref=dst, send_sem=send_sem.at[sid], recv_sem=recv_sem.at[rid], device_id=where, device_id_type=MESH)
        copy.start()
        return copy

    def got(dst, rid):
        pltpu.make_async_remote_copy(src_ref=dst, dst_ref=dst, send_sem=send_sem.at[0], recv_sem=recv_sem.at[rid], device_id={"c": other}, device_id_type=MESH).wait_recv()

    places = [
        (wup_ref.at[0], Q3.at[0]),
        (act_ref.at[pl.ds(z * WIDE, WIDE), :], X),
        (wdn_ref.at[0], W.at[1, z]),
        (wup_ref.at[1], Q3.at[1]),
        (wdn_ref.at[1], W.at[TRIO, z]),
        (dy_ref.at[pl.ds(z * WIDE, WIDE), :], DY),
    ]
    for k, ref in enumerate((up_ref_a, up_ref_b, up_ref_c)):
        places.append((ref, SUP.at[k]))
    for k, ref in enumerate((down_ref_a, down_ref_b, down_ref_c)):
        places.append((ref, SDN.at[k]))
    loads = [pltpu.make_async_copy(src, dst, local_sem.at[i]) for i, (src, dst) in enumerate(places)]
    for copy in loads:
        copy.start()

    barrier = pltpu.get_barrier_semaphore()
    for d in range(1, EIGHT):
        pl.semaphore_signal(barrier, inc=1, device_id={"z": (z + d) % EIGHT}, device_id_type=MESH)
    flat_me = y * EIGHT + x * PAIR + c

    def flat_device(k):
        return {"y": k // EIGHT, "x": (k // PAIR) % FOUR, "c": k % PAIR}

    def flat_body(d, _):
        pl.semaphore_signal(barrier, inc=1, device_id=flat_device((flat_me + d) % HALFROW), device_id_type=MESH)
        return 0

    lax.fori_loop(1, HALFROW, flat_body, 0)

    zr, zl = (z + 1) % EIGHT, (z + SEVEN) % EIGHT

    class WRing:
        def __init__(self, m):
            self.m = m
            self.rids = [recv_id() for _ in range(FOUR)]
            self.lids = [recv_id() for _ in range(FOUR)]
            self.dids = [recv_id() for _ in range(SEVEN)]
            self.sent = []

        def piece(self, idx, lo=0, n=HALF):
            return W.at[self.m, idx, pl.ds(c * HALF + lo, n), :]

        def far(self, idx):
            return W.at[self.m, idx, pl.ds(other * HALF, HALF), :]

        def push(self, idx, lo, n, rid, where):
            p = self.piece(idx, lo, n)
            self.sent.append(send(p, p, rid, where))

        def start(self):
            self.push(z, 0, HALF, self.rids[0], {"z": zr})
            self.push(z, 0, HALF, self.lids[0], {"z": zl})

        def step(self, s):
            if s < TRIO:
                a, b = (z + SEVEN - s) % EIGHT, (z + 1 + s) % EIGHT
                got(self.piece(a), self.rids[s])
                if s < PAIR:
                    self.push(a, 0, HALF, self.rids[s + 1], {"z": zr})
                else:
                    self.push(a, 0, HALFROW, self.rids[TRIO], {"z": zr})
                self.push(a, 0, HALF, self.dids[PAIR * s], {"c": other})
                got(self.piece(b), self.lids[s])
                if s < PAIR:
                    self.push(b, 0, HALF, self.lids[s + 1], {"z": zl})
                else:
                    self.push(b, HALFROW, HALFROW, self.lids[TRIO], {"z": zl})
                self.push(b, 0, HALF, self.dids[PAIR * s + 1], {"c": other})
            else:
                a = (z + FOUR) % EIGHT
                got(self.piece(a, 0, HALFROW), self.rids[TRIO])
                got(self.piece(a, HALFROW, HALFROW), self.lids[TRIO])
                self.push(a, 0, HALF, self.dids[SIX], {"c": other})

        def near(self, s):
            if s < TRIO:
                a, b = (z + SEVEN - s) % EIGHT, (z + 1 + s) % EIGHT
                got(self.far(a), self.dids[PAIR * s])
                got(self.far(b), self.dids[PAIR * s + 1])
                return [a, b]
            a = (z + FOUR) % EIGHT
            got(self.far(a), self.dids[SIX])
            return [a]

    class Rs4:
        def __init__(self, axis, me, src, one, two):
            self.axis, self.src, self.one, self.two = axis, src, one, two
            self.me, self.r, self.l, self.o = me, (me + 1) % FOUR, (me + TRIO) % FOUR, (me + PAIR) % FOUR
            self.ids = [recv_id() for _ in range(SIX)]
            self.sent = []

        def start(self):
            right, left = {self.axis: self.r}, {self.axis: self.l}
            self.sent.append(send(self.src(self.o, 0), self.one(0), self.ids[0], right))
            self.sent.append(send(self.src(self.o, 1), self.one(1), self.ids[1], left))
            self.sent.append(send(self.src(self.r, 1), self.two(0, 1), self.ids[TRIO], right))
            self.sent.append(send(self.src(self.l, 0), self.two(1, 0), self.ids[FOUR], left))

        def mid(self):
            got(self.one(0), self.ids[0])
            mine = self.src(self.r, 0)
            mine[...] = mine[...] + self.one(0)[...]
            self.sent.append(send(mine, self.two(0, 0), self.ids[PAIR], {self.axis: self.r}))
            got(self.one(1), self.ids[1])
            mine = self.src(self.l, 1)
            mine[...] = mine[...] + self.one(1)[...]
            self.sent.append(send(mine, self.two(1, 1), self.ids[5], {self.axis: self.l}))

        def fin(self, h):
            got(self.two(0, h), self.ids[PAIR + h])
            got(self.two(1, h), self.ids[FOUR + h])
            return self.src(self.me, h)[...] + self.two(0, h)[...] + self.two(1, h)[...]

    class Ag4:
        def __init__(self, axis, me, buf):
            self.axis, self.buf = axis, buf
            self.me, self.r, self.l, self.o = me, (me + 1) % FOUR, (me + TRIO) % FOUR, (me + PAIR) % FOUR
            self.ids = [recv_id() for _ in range(SIX)]
            self.sent = []

        def push(self, j, h, rid, to):
            p = self.buf(j, h)
            self.sent.append(send(p, p, rid, {self.axis: to}))

        def start(self):
            self.push(self.me, 0, self.ids[0], self.r)
            self.push(self.me, 1, self.ids[TRIO], self.l)
            self.push(self.me, 1, self.ids[1], self.r)
            self.push(self.me, 0, self.ids[PAIR], self.l)

        def fwd(self):
            got(self.buf(self.l, 0), self.ids[0])
            self.push(self.l, 0, self.ids[FOUR], self.r)
            got(self.buf(self.r, 1), self.ids[TRIO])
            self.push(self.r, 1, self.ids[5], self.l)

        def fin(self):
            got(self.buf(self.l, 1), self.ids[1])
            got(self.buf(self.r, 0), self.ids[PAIR])
            got(self.buf(self.o, 0), self.ids[FOUR])
            got(self.buf(self.o, 1), self.ids[5])

    def done(*things):
        for thing in things:
            for copy in thing.sent:
                copy.wait_send()
            thing.sent = []

    def rows_of(ref, p):
        return ref[p].reshape(SPAN, WIDE)

    def first_slice(j):
        def body(i, _):
            rows = pl.ds(pl.multiple_of(i * TILE, TILE), TILE)
            low = nt(X[rows, :], W[0, j]).astype(BF16)
            Z1[j, rows, :] = low
            A1[j, rows, :] = gelu_val(low.astype(F32)).astype(BF16)
            return 0

        lax.fori_loop(0, FOUR, body, 0)

    def partial(p, lhs, m):
        def body(n, _):
            cols = pl.ds(pl.multiple_of(n * TILE, TILE), TILE)
            rhs = W[m, :, :, cols].reshape(WIDE, TILE)
            left = jnp.concatenate([lhs[k, p * SPAN:(p + 1) * SPAN, :] for k in range(EIGHT)], axis=1)
            PART[p, :, :, cols] = nn(left, rhs).reshape(FOUR, LANE, TILE)
            return 0

        lax.fori_loop(0, FOUR, body, 0)

    def err_three(p):
        def body(n, _):
            val = nt(DY[p * SPAN:(p + 1) * SPAN, :], W[TRIO, pl.ds(PAIR * n, PAIR)].reshape(TILE, WIDE)).astype(BF16)
            Q3[PAIR * n, p * SPAN:(p + 1) * SPAN, :] = val[:, :LANE]
            Q3[PAIR * n + 1, p * SPAN:(p + 1) * SPAN, :] = val[:, LANE:]
            return 0

        lax.fori_loop(0, FOUR, body, 0)

    def block_two(p):
        def body(n, _):
            low = nt(rows_of(H, p), W[PAIR, pl.ds(PAIR * n, PAIR)].reshape(TILE, WIDE)).astype(BF16)
            for k in range(PAIR):
                part = low[:, k * LANE:(k + 1) * LANE].astype(F32)
                val, slope = gelu_both(part)
                A3[PAIR * n + k, p * SPAN:(p + 1) * SPAN, :] = val.astype(BF16)
                err = Q3[PAIR * n + k, p * SPAN:(p + 1) * SPAN, :].astype(F32)
                Q3[PAIR * n + k, p * SPAN:(p + 1) * SPAN, :] = (err * slope).astype(BF16)
            return 0

        lax.fori_loop(0, FOUR, body, 0)

    def back_one(p):
        def body(n, _):
            low = nt(rows_of(E2, p), W[1, pl.ds(PAIR * n, PAIR)].reshape(TILE, WIDE)).astype(BF16)
            for k in range(PAIR):
                zed = Z1[PAIR * n + k, p * SPAN:(p + 1) * SPAN, :].astype(F32)
                _, slope = gelu_both(zed)
                err = low[:, k * LANE:(k + 1) * LANE].astype(F32)
                Z3[PAIR * n + k, p * SPAN:(p + 1) * SPAN, :] = (err * slope).astype(BF16)
            return 0

        lax.fori_loop(0, FOUR, body, 0)

    def weight_grad(slot, hid, lo, size, other_side, down, first, last, add):
        def body(step, _):
            n = step // PAIR
            half = step % PAIR
            cols = pl.ds(pl.multiple_of(n * TILE, TILE), TILE)
            right = other_side(cols)
            for q in range(PAIR):
                base = half * FOUR + q * PAIR
                left = jnp.concatenate([hid[base, lo:lo + size, :], hid[base + 1, lo:lo + size, :]], axis=1)
                val = tn(left, right)
                for k in range(PAIR):
                    blk = val[k * LANE:(k + 1) * LANE, :]
                    for e in range(PAIR):
                        sub = blk[:, e * LANE:(e + 1) * LANE]
                        if down:
                            lane = pl.ds(pl.multiple_of((PAIR * n + e) * SUB, SUB), SUB)
                            for b in range(EIGHT):
                                old = G[slot, base + k, b // PAIR, b % PAIR, lane, :] if add else 0.0
                                G[slot, base + k, b // PAIR, b % PAIR, lane, :] = old + sub[b * SUB:(b + 1) * SUB, :]
                        else:
                            old = G[slot, base + k, n, e] if add else 0.0
                            G[slot, base + k, n, e] = old + sub
            return 0

        lax.fori_loop(PAIR * first, PAIR * last, body, 0)

    class GradPart:
        def __init__(self, k, u):
            self.k, self.u, self.slot = k, u, k % PAIR
            self.did = recv_id()
            self.zid = recv_id()
            slot = self.slot
            rows = pl.ds(HALF * u, HALF)
            self.rows = rows
            self.rs = Rs4("x", x, lambda j, h: G.at[slot, pl.ds(FOUR * h, FOUR), j, c, rows], lambda d: X1.at[k, u, d], lambda d, h: X2.at[k, u, d, h])
            self.sent = []
            self.zsent = []

        def d2d(self):
            if self.k >= PAIR:
                pl.semaphore_wait(credit.at[self.slot, self.u], 1)
            self.sent.append(send(G.at[self.slot, :, :, other, self.rows], DD.at[self.slot, self.u], self.did, {"c": other}))

        def xs(self):
            got(DD.at[self.slot, self.u], self.did)
            slot, u, rows = self.slot, self.u, self.rows

            def body(i, _):
                mine = G.at[slot, i, :, c, rows]
                mine[...] = mine[...] + DD[slot, u, i]
                return 0

            lax.fori_loop(0, EIGHT, body, 0)
            if self.k < PAIR:
                pl.semaphore_signal(credit.at[slot, u], inc=1, device_id={"c": other}, device_id_type=MESH)
            self.rs.start()

        def xm(self):
            self.rs.mid()

        def xf(self):
            for h in range(PAIR):
                ZS[self.slot, self.u, FOUR * h:FOUR * h + FOUR] = self.rs.fin(h)
            for d in (FOUR, TRIO, 5, PAIR, SIX, 1, SEVEN):
                to = (z + d) % EIGHT
                self.zsent.append(send(ZS.at[self.slot, self.u, to], ZR.at[self.k, self.u, d - 1], self.zid, {"z": to}))

        def zf(self):
            got(ZR.at[self.k, self.u], self.zid)
            total = ZS[self.slot, self.u, z]
            for d in range(SEVEN):
                total = total + ZR[self.k, self.u, d]
            total = total * 0.125
            GOUT[self.k, self.rows, :] = total
            sq = total * total
            return jnp.sum(sq.reshape(EIGHT, EIGHT, LANE), axis=0)

        def free_g(self):
            done(self, self.rs)

        def free_z(self):
            for copy in self.zsent:
                copy.wait_send()
            self.zsent = []

    w1, w2, w3, w4 = (WRing(m) for m in range(FOUR))
    rs_h = [Rs4("y", y, lambda j, h, p=p: PART.at[p, j, pl.ds(HALF * h, HALF), :], lambda d, p=p: Y1.at[0, p, d], lambda d, h, p=p: Y2.at[0, p, d, h]) for p in range(PAIR)]
    rs_e = [Rs4("y", y, lambda j, h, p=p: PART.at[p, j, pl.ds(HALF * h, HALF), :], lambda d, p=p: Y1.at[1, p, d], lambda d, h, p=p: Y2.at[1, p, d, h]) for p in range(PAIR)]
    ag_h = [Ag4("y", y, lambda j, h, p=p: H.at[p, j, pl.ds(HALF * h, HALF), :]) for p in range(PAIR)]
    ag_e = [Ag4("y", y, lambda j, h, p=p: E2.at[p, j, pl.ds(HALF * h, HALF), :]) for p in range(PAIR)]
    gs = [[GradPart(k, u) for u in range(PAIR)] for k in range(FOUR)]

    loads[0].wait()
    W[0, z] = Q3[0].T
    loads[1].wait()
    first_slice(z)
    loads[PAIR].wait()
    pl.semaphore_wait(barrier, 38)
    w1.start()
    w2.start()
    loads[TRIO].wait()
    W[PAIR, z] = Q3[1].T
    loads[FOUR].wait()
    for s in range(FOUR):
        w1.step(s)
        w2.step(s)
        if s == PAIR:
            w3.start()
            w4.start()
        for j in w1.near(s):
            first_slice(j)
    for s in range(FOUR):
        w2.near(s)
    partial(0, A1, 1)
    rs_h[0].start()
    w3.step(0)
    w4.step(0)
    partial(1, A1, 1)
    rs_h[1].start()
    w3.step(1)
    w4.step(1)
    rs_h[0].mid()
    w3.step(PAIR)
    w4.step(PAIR)
    loads[5].wait()
    rs_h[1].mid()
    w3.step(TRIO)
    w4.step(TRIO)
    for s in range(FOUR):
        w4.near(s)
    err_three(0)
    for h in range(PAIR):
        H[0, y, HALF * h:HALF * h + HALF, :] = rs_h[0].fin(h).astype(BF16)
    ag_h[0].start()
    err_three(1)
    for s in range(FOUR):
        w3.near(s)
    for h in range(PAIR):
        H[1, y, HALF * h:HALF * h + HALF, :] = rs_h[1].fin(h).astype(BF16)
    ag_h[0].fwd()
    ag_h[1].start()
    ag_h[0].fin()
    block_two(0)
    ag_h[1].fwd()
    done(rs_h[0])
    partial(0, Q3, PAIR)
    rs_e[0].start()
    ag_h[1].fin()
    block_two(1)
    done(rs_h[1])
    partial(1, Q3, PAIR)
    rs_e[1].start()
    rs_e[0].mid()
    weight_grad(0, A3, 0, WIDE, lambda cols: DY[:, cols], True, 0, PAIR, False)
    gs[0][0].d2d()
    weight_grad(0, A3, 0, WIDE, lambda cols: DY[:, cols], True, PAIR, FOUR, False)
    gs[0][1].d2d()
    gs[0][0].xs()
    weight_grad(1, Q3, 0, WIDE, lambda cols: H[:, :, :, cols].reshape(WIDE, TILE), False, 0, FOUR, False)
    gs[0][1].xs()
    gs[1][0].d2d()
    gs[1][1].d2d()
    rs_e[1].mid()
    gs[0][0].xm()
    gs[0][1].xm()
    gs[1][0].xs()
    gs[1][1].xs()
    for h in range(PAIR):
        E2[0, y, HALF * h:HALF * h + HALF, :] = rs_e[0].fin(h).astype(BF16)
    ag_e[0].start()
    gs[0][0].xf()
    gs[0][1].xf()
    for h in range(PAIR):
        E2[1, y, HALF * h:HALF * h + HALF, :] = rs_e[1].fin(h).astype(BF16)
    ag_e[0].fwd()
    ag_e[1].start()
    gs[1][0].xm()
    gs[1][1].xm()
    gs[0][0].free_g()
    gs[0][1].free_g()
    ag_e[0].fin()
    back_one(0)
    ag_e[1].fwd()
    weight_grad(0, A1, 0, SPAN, lambda cols: E2[0, :, :, cols].reshape(SPAN, TILE), True, 0, FOUR, False)
    gs[1][0].xf()
    gs[1][1].xf()
    gs[1][0].free_g()
    gs[1][1].free_g()
    weight_grad(1, Z3, 0, SPAN, lambda cols: X[:SPAN, cols], False, 0, FOUR, False)
    ag_e[1].fin()
    weight_grad(0, A1, SPAN, SPAN, lambda cols: E2[1, :, :, cols].reshape(SPAN, TILE), True, 0, PAIR, True)
    gs[PAIR][0].d2d()
    weight_grad(0, A1, SPAN, SPAN, lambda cols: E2[1, :, :, cols].reshape(SPAN, TILE), True, PAIR, FOUR, True)
    gs[PAIR][1].d2d()
    gs[PAIR][0].xs()
    back_one(1)
    gs[PAIR][1].xs()
    weight_grad(1, Z3, SPAN, SPAN, lambda cols: X[SPAN:, cols], False, 0, FOUR, True)
    gs[TRIO][0].d2d()
    gs[TRIO][1].d2d()
    gs[PAIR][0].xm()
    gs[TRIO][0].xs()
    gs[TRIO][1].xs()
    gs[PAIR][1].xm()
    sq = gs[0][0].zf() + gs[0][1].zf()
    gs[0][0].free_z()
    gs[0][1].free_z()
    gs[PAIR][0].xf()
    gs[TRIO][0].xm()
    gs[PAIR][1].xf()
    gs[TRIO][1].xm()
    sq = sq + gs[1][0].zf() + gs[1][1].zf()
    gs[1][0].free_z()
    gs[1][1].free_z()
    gs[TRIO][0].xf()
    sq = sq + gs[PAIR][0].zf()
    gs[TRIO][1].xf()
    sq = sq + gs[PAIR][1].zf() + gs[TRIO][0].zf()
    sq = sq + gs[TRIO][1].zf()

    grad_copy = pltpu.make_async_copy(GOUT, grad_out_ref, local_sem.at[0])
    grad_copy.start()
    nid, mid = recv_id(), recv_id()
    norm_sent = []
    NSRC[0] = sq
    for d in (FOUR, TRIO, 5, PAIR, SIX, 1, SEVEN):
        norm_sent.append(send(NSRC.at[0], NRCV.at[z], nid, {"z": (z + d) % EIGHT}))
    got(NRCV.at[pl.ds(0, SEVEN)], nid)
    NRCV[z] = sq
    part = NRCV[0]
    for k in range(1, EIGHT):
        part = part + NRCV[k]
    row = jnp.sum(part, axis=0, keepdims=True)
    row = jnp.broadcast_to(row, (EIGHT, LANE))
    NSRC[1] = row
    for d in range(1, HALFROW):
        norm_sent.append(send(NSRC.at[1], NRCW.at[flat_me], mid, flat_device((flat_me + d) % HALFROW)))
    got(NRCW.at[pl.ds(0, 31)], mid)
    NRCW[flat_me] = row
    total = jnp.sum(jnp.sum(NRCW[...], axis=0)[:1, :], axis=1, keepdims=True)
    norm_val = jnp.sqrt(total)
    NOUT[...] = jnp.broadcast_to(norm_val, (EIGHT, LANE))
    norm_copy = pltpu.make_async_copy(NOUT, norm_out_ref, local_sem.at[1])
    norm_copy.start()
    clip_scale = jnp.minimum(1.0, clip_ref[0] / (norm_val + NORM_EPS))
    lr_val = lr_ref[0]
    for copy in loads[SIX:]:
        copy.wait()
    for k in range(PAIR):
        new_master, _, _ = adam_update(SUP[0, k], SUP[1, k], SUP[PAIR, k], GOUT[TRIO - PAIR * k].T, clip_scale, lr_val)
        NW[x, c, k] = new_master.astype(BF16)
        flat = flatten(GOUT[PAIR - PAIR * k])
        new_master, _, _ = adam_update(SDN[0, k], SDN[1, k], SDN[PAIR, k], flat, clip_scale, lr_val)
        low = new_master.astype(BF16)
        for e in range(EIGHT):
            NW[x, c, PAIR + k, e * SUB:(e + 1) * SUB, :] = low[:, e * LANE:(e + 1) * LANE]
    ag_w = Ag4("x", x, lambda j, h: NW.at[j, c, pl.ds(PAIR * h, PAIR)])
    ag_w.start()
    pair = [recv_id() for _ in range(FOUR)]
    last = []

    def across(i, j):
        last.append(send(NW.at[j, c], NW.at[j, c], pair[i], {"c": other}))

    across(0, x)
    ag_w.fwd()
    ag_w.fin()
    for i, j in ((1, ag_w.l), (PAIR, ag_w.r), (TRIO, ag_w.o)):
        across(i, j)
    for i, j in ((0, x), (1, ag_w.l), (PAIR, ag_w.r), (TRIO, ag_w.o)):
        got(NW.at[j, other], pair[i])
    weight_copy = pltpu.make_async_copy(NW, weight_out_ref, local_sem.at[PAIR])
    weight_copy.start()

    for copy in last + norm_sent:
        copy.wait_send()
    done(w1, w2, w3, w4, ag_w, *rs_e, *ag_h, *ag_e)
    for parts in gs[PAIR:]:
        for part in parts:
            part.free_g()
            part.free_z()
    for copy in (grad_copy, norm_copy, weight_copy):
        copy.wait()


def flatten(grad):
    return jnp.concatenate([grad[e * SUB:(e + 1) * SUB, :] for e in range(EIGHT)], axis=1)


def finish_kernel(grad, norm, low, mau, mad, mou, mod, vau, vad, lr_ref, clip_ref, nwu, nwd, omau, omad, omou, omod, ovau, ovad, onorm):
    norm_val = norm[:1, :1]
    onorm[...] = norm_val
    clip_scale = jnp.minimum(1.0, clip_ref[0] / (norm_val + NORM_EPS))
    lr_val = lr_ref[0]
    for k in range(PAIR):
        omau[k], omou[k], ovau[k] = adam_update(mau[k], mou[k], vau[k], grad[TRIO - PAIR * k].T, clip_scale, lr_val)
        omad[k], omod[k], ovad[k] = adam_update(mad[k], mod[k], vad[k], flatten(grad[PAIR - PAIR * k]), clip_scale, lr_val)
        for b in range(EIGHT):
            nwu[k, b * LANE:(b + 1) * LANE, :] = low[b // PAIR, b % PAIR, k]
            nwd[k, b * SUB:(b + 1) * SUB, :] = flatten(low[b // PAIR, b % PAIR, PAIR + k])


SENDS = 330
RECVS = 250


def fused_step(act_in, grad_out, w_up, w_down, states, scalars):
    anywhere = pl.BlockSpec(memory_space=pl.ANY)
    near = pl.BlockSpec(memory_space=pltpu.VMEM)
    scalar = pl.BlockSpec(memory_space=pltpu.SMEM)
    act = pltpu.VMEM((EIGHT, WIDE, LANE), BF16)
    rows = pltpu.VMEM((PAIR, FOUR, LANE, WIDE), BF16)
    scratch = [
        pltpu.VMEM((WIDE, WIDE), BF16),
        pltpu.VMEM((WIDE, WIDE), BF16),
        pltpu.VMEM((FOUR, EIGHT, LANE, WIDE), BF16),
        act, act, act, act,
        rows, rows,
        act,
        pltpu.VMEM((PAIR, FOUR, LANE, WIDE), F32),
        pltpu.VMEM((PAIR, PAIR, PAIR, HALF, WIDE), F32),
        pltpu.VMEM((PAIR, PAIR, PAIR, PAIR, HALF, WIDE), F32),
        pltpu.VMEM((PAIR, EIGHT, FOUR, PAIR, LANE, LANE), F32),
        pltpu.VMEM((PAIR, PAIR, EIGHT, FOUR, HALF, LANE), F32),
        pltpu.VMEM((FOUR, PAIR, PAIR, FOUR, HALF, LANE), F32),
        pltpu.VMEM((FOUR, PAIR, PAIR, PAIR, FOUR, HALF, LANE), F32),
        pltpu.VMEM((PAIR, PAIR, EIGHT, HALF, LANE), F32),
        pltpu.VMEM((FOUR, PAIR, SEVEN, HALF, LANE), F32),
        pltpu.VMEM((FOUR, PAIR, FOUR, LANE, LANE), BF16),
        pltpu.VMEM((PAIR, EIGHT, LANE), F32),
        pltpu.VMEM((EIGHT, EIGHT, LANE), F32),
        pltpu.VMEM((HALFROW, EIGHT, LANE), F32),
        pltpu.VMEM((TRIO, PAIR, LANE, LANE), F32),
        pltpu.VMEM((TRIO, PAIR, SUB, WIDE), F32),
        pltpu.VMEM((FOUR, LANE, LANE), F32),
        pltpu.VMEM((EIGHT, LANE), F32),
        pltpu.SemaphoreType.DMA((12,)),
        pltpu.SemaphoreType.DMA((SENDS,)),
        pltpu.SemaphoreType.DMA((RECVS,)),
        pltpu.SemaphoreType.REGULAR((PAIR, PAIR)),
    ]
    up = jax.ShapeDtypeStruct((PAIR, LANE, LANE), F32)
    down = jax.ShapeDtypeStruct((PAIR, SUB, WIDE), F32)
    mau, mad, mou, mod, vau, vad = states
    grad, norm, low = pl.pallas_call(
        kernel,
        out_shape=(jax.ShapeDtypeStruct((FOUR, LANE, LANE), F32), jax.ShapeDtypeStruct((EIGHT, LANE), F32), jax.ShapeDtypeStruct((FOUR, PAIR, FOUR, LANE, LANE), BF16)),
        in_specs=[anywhere] * 10 + [scalar] * PAIR,
        out_specs=(anywhere, anywhere, anywhere),
        scratch_shapes=scratch,
        compiler_params=pltpu.CompilerParams(collective_id=0, has_side_effects=True, vmem_limit_bytes=VMEM_LIMIT),
        name="fused_step",
    )(act_in, grad_out, w_up, w_down, mau, mou, vau, mad, mod, vad, *scalars)
    return pl.pallas_call(
        finish_kernel,
        out_shape=(jax.ShapeDtypeStruct((PAIR, WIDE, LANE), BF16), jax.ShapeDtypeStruct((PAIR, LANE, WIDE), BF16), up, down, up, down, up, down, jax.ShapeDtypeStruct((1, 1), F32)),
        in_specs=[near] * 9 + [scalar] * PAIR,
        out_specs=tuple([near] * 9),
        name="finish",
    )(grad, norm, low, *states, *scalars)


def solution(mesh):
    big = Mesh(mesh.devices.reshape(EIGHT, FOUR, FOUR, PAIR), ("z", "y", "x", "c"))
    model = ("z", "y")
    data = ("x", "c")
    spec_rows = P(data, None)
    spec_wup = P(None, None, model)
    spec_wdown = P(None, model, None)
    spec_sup = P(None, data, model)
    spec_sdown = P(None, model + data, None)
    spec_scalar = P(None)

    def local_step(act_in, grad_out, w_up, w_down, master_up, master_down, mom_up, mom_down, var_up, var_down, learn_rate, clip_norm):
        states = (master_up, master_down, mom_up, mom_down, var_up, var_down)
        outs = fused_step(act_in, grad_out, w_up, w_down, states, (learn_rate, clip_norm))
        return outs[:EIGHT] + (outs[EIGHT].reshape(1),)

    return jax.shard_map(local_step, mesh=big, in_specs=(spec_rows, spec_rows, spec_wup, spec_wdown, spec_sup, spec_sdown, spec_sup, spec_sdown, spec_sup, spec_sdown, spec_scalar, spec_scalar), out_specs=(spec_wup, spec_wdown, spec_sup, spec_sdown, spec_sup, spec_sdown, spec_sup, spec_sdown, spec_scalar), check_vma=False)
```

time: 1090 us -> 228 us (0.21)
  waiting for transfers between devices: 846 us -> 0 us
  Pallas kernels: 0 us -> 225 us
  blocking collectives: 106 us -> 0 us
  matrix products: 56.7 us -> 0 us
  local copies, waits for them, and re-layouts: 44 us -> 0 us
  between operations: 19.1 us -> 2.04 us
    reduce_scatter x6 -> x0, waiting for transfers between devices: 638 us -> none  [the longest x2 292 us: red_down(): return lax.psum_scatter(grad, every, scatter_dimension=0, tiled=True)]
    pallas_call x0 -> x2, Pallas kernels: none -> 225 us  [the longest x1 223 us: fused_step(): pl.pallas_call(kernel, out_shape=(jax.ShapeDtypeStruct((FOUR, LANE, LANE)...]
    all_gather x6 -> x0, waiting for transfers between devices: 207 us -> none  [the longest x2 51.1 us: sum_rows(): return lax.all_gather(mine, 'y', axis=0, tiled=True)]
    psum x1 -> x0, blocking collectives: 79.6 us -> none  [local_step(): norm_val = jnp.sqrt(lax.psum(sq_local, ('z', 'y', 'x', 'c')))]
    dot_general x9 -> x0, matrix products: 56.7 us -> none  [the longest x4 28.3 us: dot_tn(): lax.dot_general(left, right, (((0,), (0,)), ((), ())), preferred_element_...]
    all_gather x2 -> x0, blocking collectives: 26.7 us -> none  [the longest x1 13.6 us: local_step(): lax.all_gather(new_master_up.astype(BF16), data, axis=1, tiled=True)]
    unnamed x32 -> x0, local copies, waits for them, and re-layouts: 24.9 us -> none
    transpose x4 -> x0, local copies, waits for them, and re-layouts: 15.4 us -> none  [red_up(): grad.reshape(8, 128, 8, 128).transpose(0, 2, 1, 3).reshape(64 * 128, 128)]
  transfers between devices with their start and end apart: 12 -> 0, of which waited for: 12 -> 0; matrix products, arithmetic and copies ran while one was open for 7% -> 0% of each run, Pallas kernels for 0% -> 0%
where the time goes in v2:
time: 228 us
  Pallas kernels  225 us (99%)
    pallas_call x1, Pallas kernels, fused_step(): pl.pallas_call(kernel, out_shape=(jax.ShapeDtypeStruct((FOUR, LANE, LANE)...  223 us

profile of v2, /device:TPU:1, one launch (start us, length us, event | category | flops | bytes accessed | tf_op | source)
XLA Modules:
  0.0 227.5 jit_solution(8519175044312145472)
XLA Ops:
  1.9 222.5 %fused_step.1 = (f32[4,128,128]{2,1,0:T(8,128)}, f32[8,128]{1,0:T(8,128)}, bf16[4,2,4,128,128]{4,3,2,1,0:T(8,128)(2,1)}) custom-call(bf16[8192,1024]{1,0:T(8,128)(2,1)} %act_ref.1, bf16[8192,1024]{1,0:T(8,128)(2,1)} %dy_ref.1, bf16[2,1024,128]{2,1,0:T(8,128)(2,1)} %wup_ref.1, bf16[2,128,1024]{2,1,0:T(8,128)(2,1)} %wdn_ref.1, f32[2,128,128]{2,1,0:T(8,128)} %mau.1, ...), custom_call_target="tpu_custom_call" | custom-call | tf_op jit(solution)/shard_map/fused_step/pallas_call | solution.py:646
  224.4 3.0 %finish.1 = (bf16[2,1024,128]{2,1,0:T(8,128)(2,1)}, bf16[2,128,1024]{2,1,0:T(8,128)(2,1)}, f32[2,128,128]{2,1,0:T(8,128)}, f32[2,16,1024]{2,1,0:T(8,128)}, f32[2...) custom-call(f32[4,128,128]{2,1,0:T(8,128)} %get-tuple-element.21.gra, ...), custom_call_target="tpu_custom_call" | custom-call | tf_op jit(solution)/shard_map/finish/pallas_call | solution.py:655

commit v3 on v2

--- a/solution.py
+++ b/solution.py
@@ -178,6 +178,52 @@
             got(self.far(a), self.dids[SIX])
             return [a]
 
+    class FirstRing:
+        def __init__(self):
+            self.rids = [[recv_id() for _ in range(PAIR)] for _ in range(FOUR)]
+            self.lids = [[recv_id() for _ in range(PAIR)] for _ in range(FOUR)]
+            self.dids = [recv_id() for _ in range(SEVEN)]
+            self.sent = []
+
+        def piece(self, idx, u):
+            return W.at[0, idx, pl.ds(c * HALF + u * HALFROW, HALFROW), :]
+
+        def push(self, idx, u, rid, where):
+            p = self.piece(idx, u)
+            self.sent.append(send(p, p, rid, where))
+
+        def cross(self, idx, rid):
+            p = W.at[0, idx, pl.ds(c * HALF, HALF), :]
+            self.sent.append(send(p, p, rid, {"c": other}))
+
+        def start(self, u):
+            self.push(z, u, self.rids[0][u], {"z": zr})
+            self.push(z, u, self.lids[0][u], {"z": zl})
+
+        def step(self, s):
+            if s < TRIO:
+                a, b = (z + SEVEN - s) % EIGHT, (z + 1 + s) % EIGHT
+                for u in range(PAIR):
+                    got(self.piece(a, u), self.rids[s][u])
+                    if s < PAIR or u == 0:
+                        self.push(a, u, self.rids[s + 1][u], {"z": zr})
+                    got(self.piece(b, u), self.lids[s][u])
+                    if s < PAIR or u == 1:
+                        self.push(b, u, self.lids[s + 1][u], {"z": zl})
+                self.cross(a, self.dids[PAIR * s])
+                self.cross(b, self.dids[PAIR * s + 1])
+            else:
+                a = (z + FOUR) % EIGHT
+                got(self.piece(a, 0), self.rids[s][0])
+                got(self.piece(a, 1), self.lids[s][1])
+                self.cross(a, self.dids[PAIR * s])
+
+        def near(self, s):
+            found = [(z + SEVEN - s) % EIGHT, (z + 1 + s) % EIGHT] if s < TRIO else [(z + FOUR) % EIGHT]
+            for i, j in enumerate(found):
+                got(W.at[0, j, pl.ds(other * HALF, HALF), :], self.dids[PAIR * s + i])
+            return found
+
     class Rs4:
         def __init__(self, axis, me, src, one, two):
             self.axis, self.src, self.one, self.two = axis, src, one, two
@@ -236,6 +282,57 @@
             got(self.buf(self.o, 0), self.ids[FOUR])
             got(self.buf(self.o, 1), self.ids[5])
 
+    class SharedRing:
+        def __init__(self):
+            self.rids = [recv_id() for _ in range(FOUR)]
+            self.lids = [recv_id() for _ in range(TRIO)]
+            self.dids = [recv_id() for _ in range(SEVEN)]
+            self.sent = []
+            self.ags = []
+            for s in range(FOUR):
+                if s < TRIO:
+                    pair = ((z + SEVEN - s) % EIGHT, (z + 1 + s) % EIGHT)
+                    self.ags.append(Ag4("x", x, lambda j, h, pair=pair: self.piece(pair[h], j)))
+                else:
+                    self.ags.append(Ag4("x", x, lambda j, h: W.at[1, (z + FOUR) % EIGHT, pl.ds(c * HALF + j * SUB + h * EIGHT, EIGHT), :]))
+
+        def piece(self, idx, j):
+            return W.at[1, idx, pl.ds(c * HALF + j * SUB, SUB), :]
+
+        def push(self, idx, rid, where):
+            p = self.piece(idx, x)
+            self.sent.append(send(p, p, rid, where))
+
+        def start(self):
+            self.push(z, self.rids[0], {"z": zr})
+            self.push(z, self.lids[0], {"z": zl})
+
+        def step(self, s):
+            a, b = (z + SEVEN - s) % EIGHT, (z + 1 + s) % EIGHT
+            got(self.piece(a, x), self.rids[s])
+            if s < TRIO:
+                self.push(a, self.rids[s + 1], {"z": zr})
+                got(self.piece(b, x), self.lids[s])
+                if s < PAIR:
+                    self.push(b, self.lids[s + 1], {"z": zl})
+            self.ags[s].start()
+
+        def fwd(self, s):
+            self.ags[s].fwd()
+
+        def chunks(self, s):
+            return [(z + SEVEN - s) % EIGHT, (z + 1 + s) % EIGHT] if s < TRIO else [(z + FOUR) % EIGHT]
+
+        def fin(self, s):
+            self.ags[s].fin()
+            for i, j in enumerate(self.chunks(s)):
+                p = W.at[1, j, pl.ds(c * HALF, HALF), :]
+                self.sent.append(send(p, p, self.dids[PAIR * s + i], {"c": other}))
+
+        def near(self, s):
+            for i, j in enumerate(self.chunks(s)):
+                got(W.at[1, j, pl.ds(other * HALF, HALF), :], self.dids[PAIR * s + i])
+
     def done(*things):
         for thing in things:
             for copy in thing.sent:
@@ -255,12 +352,13 @@
 
         lax.fori_loop(0, FOUR, body, 0)
 
-    def partial(p, lhs, m):
+    def partial(p, lhs, m, slices, add):
         def body(n, _):
             cols = pl.ds(pl.multiple_of(n * TILE, TILE), TILE)
-            rhs = W[m, :, :, cols].reshape(WIDE, TILE)
-            left = jnp.concatenate([lhs[k, p * SPAN:(p + 1) * SPAN, :] for k in range(EIGHT)], axis=1)
-            PART[p, :, :, cols] = nn(left, rhs).reshape(FOUR, LANE, TILE)
+            right = jnp.concatenate([W[m, i, :, cols] for i in slices], axis=0)
+            left = jnp.concatenate([lhs[i, p * SPAN:(p + 1) * SPAN, :] for i in slices], axis=1)
+            val = nn(left, right).reshape(FOUR, LANE, TILE)
+            PART[p, :, :, cols] = PART[p, :, :, cols] + val if add else val
             return 0
 
         lax.fori_loop(0, FOUR, body, 0)
@@ -326,34 +424,34 @@
         lax.fori_loop(PAIR * first, PAIR * last, body, 0)
 
     class GradPart:
-        def __init__(self, k, u):
-            self.k, self.u, self.slot = k, u, k % PAIR
+        def __init__(self, k, i, lo, size):
+            self.k, self.i, self.slot, self.size = k, i, k % PAIR, size
             self.did = recv_id()
             self.zid = recv_id()
             slot = self.slot
-            rows = pl.ds(HALF * u, HALF)
+            rows = pl.ds(lo, size)
             self.rows = rows
-            self.rs = Rs4("x", x, lambda j, h: G.at[slot, pl.ds(FOUR * h, FOUR), j, c, rows], lambda d: X1.at[k, u, d], lambda d, h: X2.at[k, u, d, h])
+            self.rs = Rs4("x", x, lambda j, h: G.at[slot, pl.ds(FOUR * h, FOUR), j, c, rows], lambda d: X1.at[k, d, :, rows], lambda d, h: X2.at[k, d, h, :, rows])
             self.sent = []
             self.zsent = []
 
         def d2d(self):
-            if self.k >= PAIR:
-                pl.semaphore_wait(credit.at[self.slot, self.u], 1)
-            self.sent.append(send(G.at[self.slot, :, :, other, self.rows], DD.at[self.slot, self.u], self.did, {"c": other}))
+            if self.k >= PAIR and self.i == 0:
+                pl.semaphore_wait(credit.at[self.slot], PAIR)
+            self.sent.append(send(G.at[self.slot, :, :, other, self.rows], DD.at[self.slot, :, :, self.rows], self.did, {"c": other}))
 
         def xs(self):
-            got(DD.at[self.slot, self.u], self.did)
-            slot, u, rows = self.slot, self.u, self.rows
+            slot, rows = self.slot, self.rows
+            got(DD.at[slot, :, :, rows], self.did)
 
             def body(i, _):
                 mine = G.at[slot, i, :, c, rows]
-                mine[...] = mine[...] + DD[slot, u, i]
+                mine[...] = mine[...] + DD[slot, i, :, rows]
                 return 0
 
             lax.fori_loop(0, EIGHT, body, 0)
             if self.k < PAIR:
-                pl.semaphore_signal(credit.at[slot, u], inc=1, device_id={"c": other}, device_id_type=MESH)
+                pl.semaphore_signal(credit.at[slot], inc=1, device_id={"c": other}, device_id_type=MESH)
             self.rs.start()
 
         def xm(self):
@@ -361,20 +459,20 @@
 
         def xf(self):
             for h in range(PAIR):
-                ZS[self.slot, self.u, FOUR * h:FOUR * h + FOUR] = self.rs.fin(h)
+                ZS[self.slot, FOUR * h:FOUR * h + FOUR, self.rows] = self.rs.fin(h)
             for d in (FOUR, TRIO, 5, PAIR, SIX, 1, SEVEN):
                 to = (z + d) % EIGHT
-                self.zsent.append(send(ZS.at[self.slot, self.u, to], ZR.at[self.k, self.u, d - 1], self.zid, {"z": to}))
+                self.zsent.append(send(ZS.at[self.slot, to, self.rows], ZR.at[self.k, d - 1, self.rows], self.zid, {"z": to}))
 
         def zf(self):
-            got(ZR.at[self.k, self.u], self.zid)
-            total = ZS[self.slot, self.u, z]
+            got(ZR.at[self.k, :, self.rows], self.zid)
+            total = ZS[self.slot, z, self.rows]
             for d in range(SEVEN):
-                total = total + ZR[self.k, self.u, d]
+                total = total + ZR[self.k, d, self.rows]
             total = total * 0.125
             GOUT[self.k, self.rows, :] = total
             sq = total * total
-            return jnp.sum(sq.reshape(EIGHT, EIGHT, LANE), axis=0)
+            return jnp.sum(sq.reshape(self.size // EIGHT, EIGHT, LANE), axis=0)
 
         def free_g(self):
             done(self, self.rs)
@@ -384,12 +482,19 @@
                 copy.wait_send()
             self.zsent = []
 
-    w1, w2, w3, w4 = (WRing(m) for m in range(FOUR))
+    w1, w2, w3, w4 = FirstRing(), SharedRing(), WRing(PAIR), WRing(TRIO)
+    every = tuple(range(EIGHT))
     rs_h = [Rs4("y", y, lambda j, h, p=p: PART.at[p, j, pl.ds(HALF * h, HALF), :], lambda d, p=p: Y1.at[0, p, d], lambda d, h, p=p: Y2.at[0, p, d, h]) for p in range(PAIR)]
     rs_e = [Rs4("y", y, lambda j, h, p=p: PART.at[p, j, pl.ds(HALF * h, HALF), :], lambda d, p=p: Y1.at[1, p, d], lambda d, h, p=p: Y2.at[1, p, d, h]) for p in range(PAIR)]
     ag_h = [Ag4("y", y, lambda j, h, p=p: H.at[p, j, pl.ds(HALF * h, HALF), :]) for p in range(PAIR)]
     ag_e = [Ag4("y", y, lambda j, h, p=p: E2.at[p, j, pl.ds(HALF * h, HALF), :]) for p in range(PAIR)]
-    gs = [[GradPart(k, u) for u in range(PAIR)] for k in range(FOUR)]
+    cuts = (
+        ((0, HALF), (HALF, HALF)),
+        ((0, HALF), (HALF, HALF)),
+        ((0, HALFROW), (HALFROW, HALFROW), (HALF, HALF)),
+        ((0, HALF), (HALF, HALFROW), (HALF + HALFROW, HALFROW)),
+    )
+    gs = [[GradPart(k, i, lo, size) for i, (lo, size) in enumerate(cuts[k])] for k in range(FOUR)]
 
     loads[0].wait()
     W[0, z] = Q3[0].T
@@ -397,26 +502,37 @@
     first_slice(z)
     loads[PAIR].wait()
     pl.semaphore_wait(barrier, 38)
-    w1.start()
     w2.start()
+    w1.start(0)
+    w1.start(1)
     loads[TRIO].wait()
     W[PAIR, z] = Q3[1].T
     loads[FOUR].wait()
     for s in range(FOUR):
+        w2.step(s)
         w1.step(s)
-        w2.step(s)
         if s == PAIR:
             w3.start()
             w4.start()
+        if s >= 1:
+            w2.fwd(s - 1)
+        if s >= PAIR:
+            w2.fin(s - PAIR)
         for j in w1.near(s):
             first_slice(j)
-    for s in range(FOUR):
+    w2.fwd(TRIO)
+    w2.fin(PAIR)
+    for s in range(TRIO):
         w2.near(s)
-    partial(0, A1, 1)
+    far = (z + FOUR) % EIGHT
+    partial(0, A1, 1, [(z + d) % EIGHT for d in (0, 1, PAIR, TRIO, 5, SIX, SEVEN)], False)
+    w2.fin(TRIO)
+    w2.near(TRIO)
+    partial(0, A1, 1, [far], True)
     rs_h[0].start()
     w3.step(0)
     w4.step(0)
-    partial(1, A1, 1)
+    partial(1, A1, 1, every, False)
     rs_h[1].start()
     w3.step(1)
     w4.step(1)
@@ -444,12 +560,12 @@
     block_two(0)
     ag_h[1].fwd()
     done(rs_h[0])
-    partial(0, Q3, PAIR)
+    partial(0, Q3, PAIR, every, False)
     rs_e[0].start()
     ag_h[1].fin()
     block_two(1)
     done(rs_h[1])
-    partial(1, Q3, PAIR)
+    partial(1, Q3, PAIR, every, False)
     rs_e[1].start()
     rs_e[0].mid()
     weight_grad(0, A3, 0, WIDE, lambda cols: DY[:, cols], True, 0, PAIR, False)
@@ -489,35 +605,48 @@
     gs[1][1].free_g()
     weight_grad(1, Z3, 0, SPAN, lambda cols: X[:SPAN, cols], False, 0, FOUR, False)
     ag_e[1].fin()
-    weight_grad(0, A1, SPAN, SPAN, lambda cols: E2[1, :, :, cols].reshape(SPAN, TILE), True, 0, PAIR, True)
+
+    def second(cols):
+        return E2[1, :, :, cols].reshape(SPAN, TILE)
+
+    weight_grad(0, A1, SPAN, SPAN, second, True, 0, 1, True)
     gs[PAIR][0].d2d()
-    weight_grad(0, A1, SPAN, SPAN, lambda cols: E2[1, :, :, cols].reshape(SPAN, TILE), True, PAIR, FOUR, True)
+    weight_grad(0, A1, SPAN, SPAN, second, True, 1, PAIR, True)
     gs[PAIR][1].d2d()
+    weight_grad(0, A1, SPAN, SPAN, second, True, PAIR, FOUR, True)
+    gs[PAIR][PAIR].d2d()
     gs[PAIR][0].xs()
+    gs[PAIR][1].xs()
     back_one(1)
-    gs[PAIR][1].xs()
+    gs[PAIR][PAIR].xs()
     weight_grad(1, Z3, SPAN, SPAN, lambda cols: X[SPAN:, cols], False, 0, FOUR, True)
-    gs[TRIO][0].d2d()
-    gs[TRIO][1].d2d()
+    for part in gs[TRIO]:
+        part.d2d()
     gs[PAIR][0].xm()
+    gs[PAIR][1].xm()
     gs[TRIO][0].xs()
+    gs[PAIR][PAIR].xm()
     gs[TRIO][1].xs()
-    gs[PAIR][1].xm()
+    gs[TRIO][PAIR].xs()
     sq = gs[0][0].zf() + gs[0][1].zf()
     gs[0][0].free_z()
     gs[0][1].free_z()
     gs[PAIR][0].xf()
+    gs[PAIR][1].xf()
     gs[TRIO][0].xm()
-    gs[PAIR][1].xf()
+    gs[PAIR][PAIR].xf()
     gs[TRIO][1].xm()
+    gs[TRIO][PAIR].xm()
     sq = sq + gs[1][0].zf() + gs[1][1].zf()
     gs[1][0].free_z()
     gs[1][1].free_z()
     gs[TRIO][0].xf()
-    sq = sq + gs[PAIR][0].zf()
+    sq = sq + gs[PAIR][0].zf() + gs[PAIR][1].zf()
     gs[TRIO][1].xf()
-    sq = sq + gs[PAIR][1].zf() + gs[TRIO][0].zf()
+    gs[TRIO][PAIR].xf()
+    sq = sq + gs[PAIR][PAIR].zf() + gs[TRIO][0].zf()
     sq = sq + gs[TRIO][1].zf()
+    sq = sq + gs[TRIO][PAIR].zf()
 
     grad_copy = pltpu.make_async_copy(GOUT, grad_out_ref, local_sem.at[0])
     grad_copy.start()
@@ -575,7 +704,7 @@
 
     for copy in last + norm_sent:
         copy.wait_send()
-    done(w1, w2, w3, w4, ag_w, *rs_e, *ag_h, *ag_e)
+    done(w1, w2, w3, w4, ag_w, *w2.ags, *rs_e, *ag_h, *ag_e)
     for parts in gs[PAIR:]:
         for part in parts:
             part.free_g()
@@ -601,8 +730,8 @@
             nwd[k, b * SUB:(b + 1) * SUB, :] = flatten(low[b // PAIR, b % PAIR, PAIR + k])
 
 
-SENDS = 330
-RECVS = 250
+SENDS = 420
+RECVS = 330
 
 
 def fused_step(act_in, grad_out, w_up, w_down, states, scalars):
@@ -622,11 +751,11 @@
         pltpu.VMEM((PAIR, PAIR, PAIR, HALF, WIDE), F32),
         pltpu.VMEM((PAIR, PAIR, PAIR, PAIR, HALF, WIDE), F32),
         pltpu.VMEM((PAIR, EIGHT, FOUR, PAIR, LANE, LANE), F32),
-        pltpu.VMEM((PAIR, PAIR, EIGHT, FOUR, HALF, LANE), F32),
-        pltpu.VMEM((FOUR, PAIR, PAIR, FOUR, HALF, LANE), F32),
-        pltpu.VMEM((FOUR, PAIR, PAIR, PAIR, FOUR, HALF, LANE), F32),
-        pltpu.VMEM((PAIR, PAIR, EIGHT, HALF, LANE), F32),
-        pltpu.VMEM((FOUR, PAIR, SEVEN, HALF, LANE), F32),
+        pltpu.VMEM((PAIR, EIGHT, FOUR, LANE, LANE), F32),
+        pltpu.VMEM((FOUR, PAIR, FOUR, LANE, LANE), F32),
+        pltpu.VMEM((FOUR, PAIR, PAIR, FOUR, LANE, LANE), F32),
+        pltpu.VMEM((PAIR, EIGHT, LANE, LANE), F32),
+        pltpu.VMEM((FOUR, SEVEN, LANE, LANE), F32),
         pltpu.VMEM((FOUR, PAIR, FOUR, LANE, LANE), BF16),
         pltpu.VMEM((PAIR, EIGHT, LANE), F32),
         pltpu.VMEM((EIGHT, EIGHT, LANE), F32),
@@ -638,7 +767,7 @@
         pltpu.SemaphoreType.DMA((12,)),
         pltpu.SemaphoreType.DMA((SENDS,)),
         pltpu.SemaphoreType.DMA((RECVS,)),
-        pltpu.SemaphoreType.REGULAR((PAIR, PAIR)),
+        pltpu.SemaphoreType.REGULAR((PAIR,)),
     ]
     up = jax.ShapeDtypeStruct((PAIR, LANE, LANE), F32)
     down = jax.ShapeDtypeStruct((PAIR, SUB, WIDE), F32)

time: 228 us -> 227 us (level)
  no operation moved by 1% of the time
where the time goes in v3:
time: 227 us; the launch traced here: 226 us
  Pallas kernels  224 us (99%)
    pallas_call x1, Pallas kernels, fused_step(): pl.pallas_call(kernel, out_shape=(jax.ShapeDtypeStruct((FOUR, LANE, LANE)...  221 us

profile of v3, /device:TPU:1, one launch (start us, length us, event | category | flops | bytes accessed | tf_op | source)
XLA Modules:
  0.0 226.4 jit_solution(707216366830092509)
XLA Ops:
  1.9 221.4 %fused_step.1 = (f32[4,128,128]{2,1,0:T(8,128)}, f32[8,128]{1,0:T(8,128)}, bf16[4,2,4,128,128]{4,3,2,1,0:T(8,128)(2,1)}) custom-call(bf16[8192,1024]{1,0:T(8,128)(2,1)} %act_ref.1, bf16[8192,1024]{1,0:T(8,128)(2,1)} %dy_ref.1, bf16[2,1024,128]{2,1,0:T(8,128)(2,1)} %wup_ref.1, bf16[2,128,1024]{2,1,0:T(8,128)(2,1)} %wdn_ref.1, f32[2,128,128]{2,1,0:T(8,128)} %mau.1, ...), custom_call_target="tpu_custom_call" | custom-call | tf_op jit(solution)/shard_map/fused_step/pallas_call | solution.py:775
  223.3 3.0 %finish.1 = (bf16[2,1024,128]{2,1,0:T(8,128)(2,1)}, bf16[2,128,1024]{2,1,0:T(8,128)(2,1)}, f32[2,128,128]{2,1,0:T(8,128)}, f32[2,16,1024]{2,1,0:T(8,128)}, f32[2...) custom-call(f32[4,128,128]{2,1,0:T(8,128)} %get-tuple-element.21.gra, ...), custom_call_target="tpu_custom_call" | custom-call | tf_op jit(solution)/shard_map/finish/pallas_call | solution.py:784
